TPU v7x, 128 devices: a whole 4x4x4 slice. The times are simulated.
128 devices in a mesh: seq: 32 (over y, z, core), batch: 4 (over x).
Axes of the slice: x: 4, y: 4, z: 4, core: 2. Of those that a mesh axis runs over, the one named last changes fastest.
Arguments:
- queries: bfloat16 [4, 4096, 4096], P('batch', 'seq'), may hold values from -130 to 130
- keys: bfloat16 [4, 4096, 1024], P('batch', 'seq'), may hold values from -4 to 4
- values: bfloat16 [4, 4096, 1024], P('batch', 'seq'), may hold values from -4 to 4
- lengths: int32 [4], P('batch'), may hold values from 2048 to 4096
- block_pos: int32 [4, 32], P('batch'), may hold values from 0 to 31, each once within a row
- w_in: bfloat16 [6144, 1024], replicated, may hold values from -0.078125 to 0.078125
- b_in: float32 [1024], replicated, may hold values from -3 to 3
- output_weight: bfloat16 [1024, 8], replicated, may hold values from -0.1875 to 0.1875
- output_bias: float32 [8], replicated, may hold values from 1 to 2
Outputs:
- grad_w_in: float32 [6144, 1024], P(('seq', 'batch'))
- grad_b_in: float32 [1024], replicated
- output_weight_gradient: float32 [1024, 8], replicated
- output_bias_gradient: float32 [8], replicated
Inputs may be any that keep to these rules, and one draw needn't show every extreme that they name: Each row of block_pos names every block 0 to 31 once.
All inputs are finite; a program needn't handle non-finite values.
Results may differ from a plain program's by a relative error of at most 0.0017.
The roundings to bfloat16 on the way count: a program that leaves them out, or rounds other values in their place, can miss the bound.
Values may be sent and summed in bfloat16 or wider, within the bound.
No kernel may reach another device: no remote copies, remote signals or barrier semaphores. Data moves between devices by JAX's collectives and lax.ppermute only.
A program may use at most 128 MiB of HBM per device.

v0:
```python
import math
import jax
import jax.numpy as jnp
from jax import lax
from jax.sharding import PartitionSpec as P


def split_up(array, dim, size):
    before, after = (array.shape[:dim], array.shape[dim + 1 :])
    return jnp.moveaxis(array.reshape(*before, size, -1, *after), dim, 0)


def sent_and_summed(array, axis, dim):
    size = lax.axis_size(axis)
    tiles = lax.all_to_all(split_up(array, dim, size), axis, 0, 0, tiled=True)
    return jnp.sum(tiles, axis=0)


def in_one(arrays, axis):
    ends = [0]
    for a in arrays:
        ends.append(ends[-1] + a.size)
    so_far = lax.psum(jnp.concatenate([a.ravel() for a in arrays]), axis)
    return tuple((so_far[b:e].reshape(a.shape) for a, b, e in zip(arrays, ends, ends[1:])))


def on_device(queries, keys, values, lengths, block_pos, w_in, b_in, output_weight, output_bias):
    q_rows = queries[0]
    k_rows = keys[0]
    v_rows = values[0]
    rows = q_rows.shape[0]
    heads_kv = output_weight.shape[1]
    head_size = k_rows.shape[1] // heads_kv
    group_index = q_rows.shape[1] // k_rows.shape[1]
    scale = 1.0 / math.sqrt(head_size)
    every_key = lax.all_gather(k_rows, "seq", axis=0, tiled=True)
    total = every_key.shape[0]
    order = block_pos[0]
    offsets = jnp.arange(rows, dtype=jnp.int32)
    key_pos = (order[:, None] * rows + offsets[None, :]).reshape(-1)
    mine = lax.axis_index("seq")
    query_pos = lax.dynamic_index_in_dim(order, mine, 0, keepdims=False) * rows + offsets
    limit = lengths[0]
    allowed = (key_pos[None, :] <= query_pos[:, None]) & (key_pos < limit)[None, :]
    query_live = (query_pos < limit).astype(jnp.float32)

    def group_mass(index, sums):
        q_part = lax.dynamic_slice_in_dim(
            q_rows, index * group_index * head_size, group_index * head_size, 1
        )
        q_part = q_part.reshape(rows, group_index, head_size)
        k_part = lax.dynamic_slice_in_dim(every_key, index * head_size, head_size, 1)
        scores = (
            jnp.einsum("qhd,kd->hqk", q_part, k_part, preferred_element_type=jnp.float32) * scale
        )
        masked = jnp.where(allowed[None], scores, -1e30)
        top = jnp.max(masked, axis=2, keepdims=True)
        weights = jnp.where(allowed[None], jnp.exp(masked - top), 0.0)
        denom = jnp.sum(weights, axis=2, keepdims=True)
        share = weights / denom * query_live[None, :, None]
        column = jnp.sum(share, axis=(0, 1))
        return lax.dynamic_update_index_in_dim(sums, column, index, 0)

    partial_value = lax.fori_loop(
        0, heads_kv, group_mass, jnp.zeros((heads_kv, total), jnp.float32)
    )
    mass = sent_and_summed(partial_value, "seq", 1)
    labels = jnp.log1p(mass).T
    features = jnp.concatenate([q_rows, k_rows, v_rows], axis=1)
    pre = jnp.dot(features, w_in, preferred_element_type=jnp.float32) + b_in
    act = jax.nn.silu(pre).astype(jnp.bfloat16)
    pred = jnp.dot(act, output_weight, preferred_element_type=jnp.float32) + output_bias
    norm = 1.0 / math.sqrt(lax.axis_size("batch") * total)
    resid = ((pred - labels) * query_live[:, None] * norm).astype(jnp.bfloat16)
    back = lax.dot_general(
        resid, output_weight, (((1,), (1,)), ((), ())), preferred_element_type=jnp.float32
    )
    sig = jax.nn.sigmoid(pre)
    delta = (back * sig * (1.0 + pre * (1.0 - sig))).astype(jnp.bfloat16)
    out_term = lax.dot_general(
        act, resid, (((0,), (0,)), ((), ())), preferred_element_type=jnp.float32
    )
    grad_b_in, output_weight_gradient, output_bias_gradient = in_one(
        (
            jnp.sum(delta.astype(jnp.float32), axis=0),
            out_term,
            jnp.sum(resid.astype(jnp.float32), axis=0),
        ),
        ("seq", "batch"),
    )
    grad_w_in = lax.psum_scatter(
        lax.dot_general(
            features, delta, (((0,), (0,)), ((), ())), preferred_element_type=jnp.float32
        ),
        ("seq", "batch"),
        scatter_dimension=0,
        tiled=True,
    )
    return (grad_w_in, grad_b_in, output_weight_gradient, output_bias_gradient)


def solution(mesh):
    return jax.shard_map(
        on_device,
        mesh=mesh,
        in_specs=(
            P("batch", "seq", None),
            P("batch", "seq", None),
            P("batch", "seq", None),
            P("batch"),
            P("batch", None),
            P(),
            P(),
            P(),
            P(),
        ),
        out_specs=(P(("seq", "batch"), None), P(), P(), P()),
        check_vma=False,
    )
```

profile of v0, /device:TPU:0, one launch (start us, length us, event | category | flops | bytes accessed | tf_op | source)
XLA Modules:
  0.0 518.8 jit_solution(12301234503528148574)
XLA Ops:
  10.8 1.6 copy.14
  15.2 50.5 %all-gather.3.cloned.1.call-done = bf16[1,4096,1024]{2,1,0:T(8,128)(2,1)} async-done(((bf16[1,128,1024]{2,1,0:T(8,128)(2,1)}), bf16[1,4096,1024]{2,1,0:T(8,128)(2,1)}) %all-gather.3.cloned.1.call-update) | async-done | bytes 8388624 | tf_op jit(solution)/shard_map/all_gather | solution.py:36
  65.7 170.6 %while.16 = (s32[]{:T(128)}, f32[8,4096]{1,0:T(8,128)}, bf16[4096,1024]{1,0:T(8,128)(2,1)}, bf16[128,4096]{0,1:T(8,128)(2,1)S(1)}, s32[128]{0:T(128)S(1)}, /*ind...) while((s32[]{:T(128)}, f32[8,4096]{1,0:T(8,128)}, ...), condition=%wide.region_4.5_spmd.clone, body=%wide.region_0.4_spmd.clone.sunk | while | flops 1097869184 | bytes 22091528 | solution.py:64
  68.4 8.6 %fusion.72 = f32[4,128,4096]{1,2,0:T(8,128)} fusion(pred[128,4096]{0,1:T(8,128)(4,1)S(1)} %compare_and_fusion.2, bf16[128,4,128]{0,2,1:T(8,128)(2,1)S(1)} %bitcast.69, bf16[4096,1024]{1,0:T(8,128)(2,1)} %get-tuple-element.300, s32[]{:T(128)S(6)} %select_n.79), kind=kOutput, calls=%fused_computation.2.clone.1 | convolution fusion | flops 545268736 | bytes 10616836 | tf_op jit(solution)/shard_map/while/body/eval_jaxpr/div | solution.py:60
  77.0 8.4 %multiply_reduce_fusion.2 = f32[4096]{0:T(1024)S(1)} fusion(f32[4,128,4096]{1,2,0:T(8,128)} %fusion.72, f32[128]{0:T(128)S(1)} %compare_convert_fusion.3, pred[128,4096]{0,1:T(8,128)(4,1)S(1)} %compare_and_fusion.2, bf16[128,4,128]{0,2,1:T(8,128)(2,1)S(1)} %bitcast.70, bf16[4096,1024]{1,0:T(8,128)(2,1)} %get-tuple-element.300, s32[]{:T(128)S(6)} %select_n.79), kind=kOutput, calls=%fused_computation.5.clone.1 | convolution fusion | flops 551551488 | bytes 10633732 | tf_op jit(solution)/shard_map/while/body/eval_jaxpr/sub | solution.py:58
  85.4 1.6 dynamic_update_slice.13
  89.7 8.6 %fusion.72 = f32[4,128,4096]{1,2,0:T(8,128)} fusion(pred[128,4096]{0,1:T(8,128)(4,1)S(1)} %compare_and_fusion.2, bf16[128,4,128]{0,2,1:T(8,128)(2,1)S(1)} %bitcast.69, bf16[4096,1024]{1,0:T(8,128)(2,1)} %get-tuple-element.300, s32[]{:T(128)S(6)} %select_n.79), kind=kOutput, calls=%fused_computation.2.clone.1 | convolution fusion | flops 545268736 | bytes 10616836 | tf_op jit(solution)/shard_map/while/body/eval_jaxpr/div | solution.py:60
  98.3 8.4 %multiply_reduce_fusion.2 = f32[4096]{0:T(1024)S(1)} fusion(f32[4,128,4096]{1,2,0:T(8,128)} %fusion.72, f32[128]{0:T(128)S(1)} %compare_convert_fusion.3, pred[128,4096]{0,1:T(8,128)(4,1)S(1)} %compare_and_fusion.2, bf16[128,4,128]{0,2,1:T(8,128)(2,1)S(1)} %bitcast.70, bf16[4096,1024]{1,0:T(8,128)(2,1)} %get-tuple-element.300, s32[]{:T(128)S(6)} %select_n.79), kind=kOutput, calls=%fused_computation.5.clone.1 | convolution fusion | flops 551551488 | bytes 10633732 | tf_op jit(solution)/shard_map/while/body/eval_jaxpr/sub | solution.py:58
  106.7 1.6 dynamic_update_slice.13
  111.0 8.6 %fusion.72 = f32[4,128,4096]{1,2,0:T(8,128)} fusion(pred[128,4096]{0,1:T(8,128)(4,1)S(1)} %compare_and_fusion.2, bf16[128,4,128]{0,2,1:T(8,128)(2,1)S(1)} %bitcast.69, bf16[4096,1024]{1,0:T(8,128)(2,1)} %get-tuple-element.300, s32[]{:T(128)S(6)} %select_n.79), kind=kOutput, calls=%fused_computation.2.clone.1 | convolution fusion | flops 545268736 | bytes 10616836 | tf_op jit(solution)/shard_map/while/body/eval_jaxpr/div | solution.py:60
  119.6 8.4 %multiply_reduce_fusion.2 = f32[4096]{0:T(1024)S(1)} fusion(f32[4,128,4096]{1,2,0:T(8,128)} %fusion.72, f32[128]{0:T(128)S(1)} %compare_convert_fusion.3, pred[128,4096]{0,1:T(8,128)(4,1)S(1)} %compare_and_fusion.2, bf16[128,4,128]{0,2,1:T(8,128)(2,1)S(1)} %bitcast.70, bf16[4096,1024]{1,0:T(8,128)(2,1)} %get-tuple-element.300, s32[]{:T(128)S(6)} %select_n.79), kind=kOutput, calls=%fused_computation.5.clone.1 | convolution fusion | flops 551551488 | bytes 10633732 | tf_op jit(solution)/shard_map/while/body/eval_jaxpr/sub | solution.py:58
  128.0 1.6 dynamic_update_slice.13
  132.4 8.6 %fusion.72 = f32[4,128,4096]{1,2,0:T(8,128)} fusion(pred[128,4096]{0,1:T(8,128)(4,1)S(1)} %compare_and_fusion.2, bf16[128,4,128]{0,2,1:T(8,128)(2,1)S(1)} %bitcast.69, bf16[4096,1024]{1,0:T(8,128)(2,1)} %get-tuple-element.300, s32[]{:T(128)S(6)} %select_n.79), kind=kOutput, calls=%fused_computation.2.clone.1 | convolution fusion | flops 545268736 | bytes 10616836 | tf_op jit(solution)/shard_map/while/body/eval_jaxpr/div | solution.py:60
  141.0 8.4 %multiply_reduce_fusion.2 = f32[4096]{0:T(1024)S(1)} fusion(f32[4,128,4096]{1,2,0:T(8,128)} %fusion.72, f32[128]{0:T(128)S(1)} %compare_convert_fusion.3, pred[128,4096]{0,1:T(8,128)(4,1)S(1)} %compare_and_fusion.2, bf16[128,4,128]{0,2,1:T(8,128)(2,1)S(1)} %bitcast.70, bf16[4096,1024]{1,0:T(8,128)(2,1)} %get-tuple-element.300, s32[]{:T(128)S(6)} %select_n.79), kind=kOutput, calls=%fused_computation.5.clone.1 | convolution fusion | flops 551551488 | bytes 10633732 | tf_op jit(solution)/shard_map/while/body/eval_jaxpr/sub | solution.py:58
  149.3 1.6 dynamic_update_slice.13
  153.7 8.6 %fusion.72 = f32[4,128,4096]{1,2,0:T(8,128)} fusion(pred[128,4096]{0,1:T(8,128)(4,1)S(1)} %compare_and_fusion.2, bf16[128,4,128]{0,2,1:T(8,128)(2,1)S(1)} %bitcast.69, bf16[4096,1024]{1,0:T(8,128)(2,1)} %get-tuple-element.300, s32[]{:T(128)S(6)} %select_n.79), kind=kOutput, calls=%fused_computation.2.clone.1 | convolution fusion | flops 545268736 | bytes 10616836 | tf_op jit(solution)/shard_map/while/body/eval_jaxpr/div | solution.py:60
  162.3 8.4 %multiply_reduce_fusion.2 = f32[4096]{0:T(1024)S(1)} fusion(f32[4,128,4096]{1,2,0:T(8,128)} %fusion.72, f32[128]{0:T(128)S(1)} %compare_convert_fusion.3, pred[128,4096]{0,1:T(8,128)(4,1)S(1)} %compare_and_fusion.2, bf16[128,4,128]{0,2,1:T(8,128)(2,1)S(1)} %bitcast.70, bf16[4096,1024]{1,0:T(8,128)(2,1)} %get-tuple-element.300, s32[]{:T(128)S(6)} %select_n.79), kind=kOutput, calls=%fused_computation.5.clone.1 | convolution fusion | flops 551551488 | bytes 10633732 | tf_op jit(solution)/shard_map/while/body/eval_jaxpr/sub | solution.py:58
  170.7 1.6 dynamic_update_slice.13
  175.0 8.6 %fusion.72 = f32[4,128,4096]{1,2,0:T(8,128)} fusion(pred[128,4096]{0,1:T(8,128)(4,1)S(1)} %compare_and_fusion.2, bf16[128,4,128]{0,2,1:T(8,128)(2,1)S(1)} %bitcast.69, bf16[4096,1024]{1,0:T(8,128)(2,1)} %get-tuple-element.300, s32[]{:T(128)S(6)} %select_n.79), kind=kOutput, calls=%fused_computation.2.clone.1 | convolution fusion | flops 545268736 | bytes 10616836 | tf_op jit(solution)/shard_map/while/body/eval_jaxpr/div | solution.py:60
  183.6 8.4 %multiply_reduce_fusion.2 = f32[4096]{0:T(1024)S(1)} fusion(f32[4,128,4096]{1,2,0:T(8,128)} %fusion.72, f32[128]{0:T(128)S(1)} %compare_convert_fusion.3, pred[128,4096]{0,1:T(8,128)(4,1)S(1)} %compare_and_fusion.2, bf16[128,4,128]{0,2,1:T(8,128)(2,1)S(1)} %bitcast.70, bf16[4096,1024]{1,0:T(8,128)(2,1)} %get-tuple-element.300, s32[]{:T(128)S(6)} %select_n.79), kind=kOutput, calls=%fused_computation.5.clone.1 | convolution fusion | flops 551551488 | bytes 10633732 | tf_op jit(solution)/shard_map/while/body/eval_jaxpr/sub | solution.py:58
  192.0 1.6 dynamic_update_slice.13
  196.3 8.6 %fusion.72 = f32[4,128,4096]{1,2,0:T(8,128)} fusion(pred[128,4096]{0,1:T(8,128)(4,1)S(1)} %compare_and_fusion.2, bf16[128,4,128]{0,2,1:T(8,128)(2,1)S(1)} %bitcast.69, bf16[4096,1024]{1,0:T(8,128)(2,1)} %get-tuple-element.300, s32[]{:T(128)S(6)} %select_n.79), kind=kOutput, calls=%fused_computation.2.clone.1 | convolution fusion | flops 545268736 | bytes 10616836 | tf_op jit(solution)/shard_map/while/body/eval_jaxpr/div | solution.py:60
  204.9 8.4 %multiply_reduce_fusion.2 = f32[4096]{0:T(1024)S(1)} fusion(f32[4,128,4096]{1,2,0:T(8,128)} %fusion.72, f32[128]{0:T(128)S(1)} %compare_convert_fusion.3, pred[128,4096]{0,1:T(8,128)(4,1)S(1)} %compare_and_fusion.2, bf16[128,4,128]{0,2,1:T(8,128)(2,1)S(1)} %bitcast.70, bf16[4096,1024]{1,0:T(8,128)(2,1)} %get-tuple-element.300, s32[]{:T(128)S(6)} %select_n.79), kind=kOutput, calls=%fused_computation.5.clone.1 | convolution fusion | flops 551551488 | bytes 10633732 | tf_op jit(solution)/shard_map/while/body/eval_jaxpr/sub | solution.py:58
  213.3 1.6 dynamic_update_slice.13
  217.6 8.6 %fusion.72 = f32[4,128,4096]{1,2,0:T(8,128)} fusion(pred[128,4096]{0,1:T(8,128)(4,1)S(1)} %compare_and_fusion.2, bf16[128,4,128]{0,2,1:T(8,128)(2,1)S(1)} %bitcast.69, bf16[4096,1024]{1,0:T(8,128)(2,1)} %get-tuple-element.300, s32[]{:T(128)S(6)} %select_n.79), kind=kOutput, calls=%fused_computation.2.clone.1 | convolution fusion | flops 545268736 | bytes 10616836 | tf_op jit(solution)/shard_map/while/body/eval_jaxpr/div | solution.py:60
  226.2 8.4 %multiply_reduce_fusion.2 = f32[4096]{0:T(1024)S(1)} fusion(f32[4,128,4096]{1,2,0:T(8,128)} %fusion.72, f32[128]{0:T(128)S(1)} %compare_convert_fusion.3, pred[128,4096]{0,1:T(8,128)(4,1)S(1)} %compare_and_fusion.2, bf16[128,4,128]{0,2,1:T(8,128)(2,1)S(1)} %bitcast.70, bf16[4096,1024]{1,0:T(8,128)(2,1)} %get-tuple-element.300, s32[]{:T(128)S(6)} %select_n.79), kind=kOutput, calls=%fused_computation.5.clone.1 | convolution fusion | flops 551551488 | bytes 10633732 | tf_op jit(solution)/shard_map/while/body/eval_jaxpr/sub | solution.py:58
  234.6 1.6 dynamic_update_slice.13
  236.2 5.5 %all-to-all-start = ((f32[32,8,128]{2,1,0:T(8,128)}), f32[32,8,128]{2,1,0:T(8,128)S(1)}, u32[]{:S(2)}, u32[]{:S(2)}) async-start(f32[32,8,128]{2,1,0:T(8,128)} %bitcast.9), calls=%async_computation | async-start | bytes 262144 | tf_op jit(solution)/shard_map/all_to_all | solution.py:15
  242.0 6.5 %multiply_convert_fusion = (bf16[128,1024]{1,0:T(8,128)(2,1)S(1)}, f32[128,1024]{1,0:T(8,128)S(1)}) fusion(f32[1024]{0:T(1024)S(1)} %copy-done.1, bf16[6144,1024]{1,0:T(8,128)(2,1)} %param.16, bf16[128,1024]{0,1:T(8,128)(2,1)S(1)} %bitcast.73, bf16[128,1024]{0,1:T(8,128)(2,1)S(1)} %bitcast.71, bf16[128,4096]{0,1:T(8,128)(2,1)S(1)} %get-tuple-element.317), kind=kOutput, calls=%fused_computation.42 | convolution fusion | flops 1616117760 | bytes 14946304 | tf_op jit(solution)/shard_map/dot_general | solution.py:70
  250.3 13.2 %fusion.46 = f32[6144,1024]{1,0:T(8,128)} fusion(bf16[128,1024]{1,0:T(8,128)(2,1)S(1)} %get-tuple-element.212, bf16[128,1024]{0,1:T(8,128)(2,1)S(1)} %bitcast.74, bf16[128,1024]{0,1:T(8,128)(2,1)S(1)} %bitcast.72, bf16[128,4096]{0,1:T(8,128)(2,1)S(1)} %get-tuple-element.317), kind=kOutput, calls=%fused_computation.40 | convolution fusion | flops 1615331328 | bytes 27000832 | tf_op jit(solution)/shard_map/dot_general | solution.py:92
  264.1 67.0 %psum.7 = f32[9224]{0:T(1024)S(1)} all-reduce(f32[9224]{0:T(1024)S(1)} %pad_maximum_fusion.3), channel_id=1, replica_groups=mesh['seq'=32,'batch'=4] {'seq','batch'}, use_global_device_ids=true, to_apply=%region_9.10 | all-reduce | flops 9224 | bytes 73792 | tf_op jit(solution)/shard_map/psum | solution.py:23
  333.2 178.8 %reduce-scatter.2.cloned.1.call-done = f32[48,1024]{1,0:T(8,128)} async-done(((f32[6144,1024]{1,0:T(8,128)}), f32[48,1024]{1,0:T(8,128)}) %reduce-scatter.2.cloned.1.call-update) | async-done | bytes 196624 | tf_op jit(solution)/shard_map/reduce_scatter | solution.py:91
  (55 shorter events, 32.0 us)
Async XLA Ops:
  7.2 242.5 %copy-start = (bf16[1024,8]{0,1:T(8,128)(2,1)S(1)}, bf16[1024,8]{0,1:T(8,128)(2,1)}, u32[]{:S(2)}) copy-start(bf16[1024,8]{0,1:T(8,128)(2,1)} %param.18) | copy-start | bytes 49156
  7.2 58.5 %all-gather.3.cloned.1.call-start = ((), (), s32[]{:S(2)}) async-start(), calls=%async_computation.3 | async-start | bytes 8650752 | tf_op jit(solution)/shard_map/all_gather | solution.py:36
  65.7 176.3 %copy-start.1 = (f32[1024]{0:T(1024)S(1)}, f32[1024]{0:T(1024)}, u32[]{:S(2)}) copy-start(f32[1024]{0:T(1024)} %param.17) | copy-start | bytes 12292
  236.2 13.3 %all-to-all-start = ((f32[32,8,128]{2,1,0:T(8,128)}), f32[32,8,128]{2,1,0:T(8,128)S(1)}, u32[]{:S(2)}, u32[]{:S(2)}) async-start(f32[32,8,128]{2,1,0:T(8,128)} %bitcast.9), calls=%async_computation | async-start | bytes 262144 | tf_op jit(solution)/shard_map/all_to_all | solution.py:15
  241.7 270.2 %reduce-scatter.2.cloned.1.call-start = ((), (), s32[]{:S(2)}) async-start(), calls=%async_computation.2 | async-start | bytes 25362432 | tf_op jit(solution)/shard_map/reduce_scatter | solution.py:91
  242.0 7.6 %copy-start.2 = (f32[8]{0:T(128)S(1)}, f32[8]{0:T(128)}, u32[]{:S(2)}) copy-start(f32[8]{0:T(128)} %param.19) | copy-start | bytes 100
Sparse Core Ops, SparseCore 0:
  10.3 55.3 all-gather.2
  263.7 248.2 reduce-scatter.1
where the time goes:
time: 520 us; the launch traced here: 519 us
  waiting for transfers between devices  230 us (44%)
  matrix products  156 us (30%)
  blocking collectives  67 us (13%)
  other arithmetic  24.9 us (5%)
  local copies, waits for them, and re-layouts  19.4 us (4%)
  between operations  14.8 us (3%)
  starting transfers between devices  5.76 us (1%)
    reduce_scatter x1, waiting for transfers between devices, on_device(): lax.psum_scatter(lax.dot_general(features, delta, (((0,), (0,)), ((), ())...  179 us
    div x8, matrix products, group_mass(): share = weights / denom * query_live[None, :, None]  68.8 us
    sub x8, matrix products, group_mass(): weights = jnp.where(allowed[None], jnp.exp(masked - top), 0.0)  67 us
    psum x1, blocking collectives, in_one(): so_far = lax.psum(jnp.concatenate([a.ravel() for a in arrays]), axis)  67 us
    all_gather x1, waiting for transfers between devices, on_device(): every_key = lax.all_gather(k_rows, 'seq', axis=0, tiled=True)  50.5 us
    dot_general x1, matrix products, on_device(): lax.dot_general(features, delta, (((0,), (0,)), ((), ())), preferred_elem...  13.2 us
    dynamic_update_slice x8, local copies, waits for them, and re-layouts, group_mass(): return lax.dynamic_update_index_in_dim(sums, column, index, 0)  12.9 us
    and x8, other arithmetic, on_device(): (key_pos[None, :] <= query_pos[:, None]) & (key_pos < limit)[None, :]  11.1 us
  transfers between devices with their start and end apart: 3, of which 3 were waited for; matrix products, arithmetic and copies ran while one was open for 3% of the time, Pallas kernels for 0%

commit v1 on v0

--- a/solution.py
+++ b/solution.py
@@ -20,7 +20,7 @@
     ends = [0]
     for a in arrays:
         ends.append(ends[-1] + a.size)
-    so_far = lax.psum(jnp.concatenate([a.ravel() for a in arrays]), axis)
+    so_far = lax.all_gather(jnp.concatenate([a.ravel() for a in arrays]), axis).sum(axis=0)
     return tuple((so_far[b:e].reshape(a.shape) for a, b, e in zip(arrays, ends, ends[1:])))
 
 

time: 520 us -> 671 us (1.29)
  waiting for transfers between devices: 230 us -> 434 us
  blocking collectives: 67 us -> 0 us
  local copies, waits for them, and re-layouts: 19.4 us -> 29.1 us
    unnamed x2 -> x4, waiting for transfers between devices: 0.7 us -> 144 us
    psum x1 -> x0, blocking collectives: 67 us -> none  [in_one(): so_far = lax.psum(jnp.concatenate([a.ravel() for a in arrays]), axis)]
    reduce_scatter x1, waiting for transfers between devices: 179 us -> 240 us  [on_device(): lax.psum_scatter(lax.dot_general(features, delta, (((0,), (0,)), ((), ())...]
    all_gather x0 -> x1, local copies, waits for them, and re-layouts: none -> 7.43 us  [in_one(): lax.all_gather(jnp.concatenate([a.ravel() for a in arrays]), axis)]
  transfers between devices with their start and end apart: 3 -> 4, of which waited for: 3 -> 4; matrix products, arithmetic and copies ran while one was open for 3% -> 6% of each run, Pallas kernels for 0% -> 0%
where the time goes in v1:
time: 671 us; the launch traced here: 670 us
  waiting for transfers between devices  434 us (65%)
  matrix products  157 us (23%)
  local copies, waits for them, and re-layouts  29.1 us (4%)
  other arithmetic  29 us (4%)
  between operations  14.5 us (2%)
    reduce_scatter x1, waiting for transfers between devices, on_device(): lax.psum_scatter(lax.dot_general(features, delta, (((0,), (0,)), ((), ())...  240 us
    unnamed x4, waiting for transfers between devices  144 us
    div x8, matrix products, group_mass(): share = weights / denom * query_live[None, :, None]  68.9 us
    sub x8, matrix products, group_mass(): weights = jnp.where(allowed[None], jnp.exp(masked - top), 0.0)  67.3 us
    all_gather x1, waiting for transfers between devices, on_device(): every_key = lax.all_gather(k_rows, 'seq', axis=0, tiled=True)  50.5 us
  transfers between devices with their start and end apart: 4, of which 4 were waited for; matrix products, arithmetic and copies ran while one was open for 6% of the time, Pallas kernels for 0%

profile of v1, /device:TPU:0, one launch (start us, length us, event | category | flops | bytes accessed | tf_op | source)
XLA Modules:
  0.0 669.9 jit_solution(6783217785189078675)
XLA Ops:
  15.2 50.5 %all-gather.4.cloned.1.call-done = bf16[1,4096,1024]{2,1,0:T(8,128)(2,1)} async-done(((bf16[1,128,1024]{2,1,0:T(8,128)(2,1)}), bf16[1,4096,1024]{2,1,0:T(8,128)(2,1)}) %all-gather.4.cloned.1.call-update) | async-done | bytes 8388624 | tf_op jit(solution)/shard_map/all_gather | solution.py:36
  65.7 171.1 %while.16 = (s32[]{:T(128)}, f32[8,4096]{1,0:T(8,128)}, bf16[4096,1024]{1,0:T(8,128)(2,1)}, bf16[128,4096]{0,1:T(8,128)(2,1)S(1)}, s32[128]{0:T(128)S(1)}, /*ind...) while((s32[]{:T(128)}, f32[8,4096]{1,0:T(8,128)}, ...), condition=%wide.region_4.5_spmd.clone, body=%wide.region_0.4_spmd.clone.sunk | while | flops 1097869184 | bytes 22091528 | solution.py:64
  68.4 8.6 %fusion.72 = f32[4,128,4096]{1,2,0:T(8,128)} fusion(pred[128,4096]{0,1:T(8,128)(4,1)S(1)} %compare_and_fusion.2, bf16[128,4,128]{0,2,1:T(8,128)(2,1)S(1)} %bitcast.69, bf16[4096,1024]{1,0:T(8,128)(2,1)} %get-tuple-element.300, s32[]{:T(128)S(6)} %select_n.79), kind=kOutput, calls=%fused_computation.2.clone.1 | convolution fusion | flops 545268736 | bytes 10616836 | tf_op jit(solution)/shard_map/while/body/eval_jaxpr/div | solution.py:60
  77.0 8.4 %multiply_reduce_fusion.2 = f32[4096]{0:T(1024)S(1)} fusion(f32[4,128,4096]{1,2,0:T(8,128)} %fusion.72, f32[128]{0:T(128)S(1)} %compare_convert_fusion.3, pred[128,4096]{0,1:T(8,128)(4,1)S(1)} %compare_and_fusion.2, bf16[128,4,128]{0,2,1:T(8,128)(2,1)S(1)} %bitcast.70, bf16[4096,1024]{1,0:T(8,128)(2,1)} %get-tuple-element.300, s32[]{:T(128)S(6)} %select_n.79), kind=kOutput, calls=%fused_computation.5.clone.1 | convolution fusion | flops 551551488 | bytes 10633732 | tf_op jit(solution)/shard_map/while/body/eval_jaxpr/sub | solution.py:58
  85.4 1.6 dynamic_update_slice.13
  89.8 8.6 %fusion.72 = f32[4,128,4096]{1,2,0:T(8,128)} fusion(pred[128,4096]{0,1:T(8,128)(4,1)S(1)} %compare_and_fusion.2, bf16[128,4,128]{0,2,1:T(8,128)(2,1)S(1)} %bitcast.69, bf16[4096,1024]{1,0:T(8,128)(2,1)} %get-tuple-element.300, s32[]{:T(128)S(6)} %select_n.79), kind=kOutput, calls=%fused_computation.2.clone.1 | convolution fusion | flops 545268736 | bytes 10616836 | tf_op jit(solution)/shard_map/while/body/eval_jaxpr/div | solution.py:60
  98.4 8.4 %multiply_reduce_fusion.2 = f32[4096]{0:T(1024)S(1)} fusion(f32[4,128,4096]{1,2,0:T(8,128)} %fusion.72, f32[128]{0:T(128)S(1)} %compare_convert_fusion.3, pred[128,4096]{0,1:T(8,128)(4,1)S(1)} %compare_and_fusion.2, bf16[128,4,128]{0,2,1:T(8,128)(2,1)S(1)} %bitcast.70, bf16[4096,1024]{1,0:T(8,128)(2,1)} %get-tuple-element.300, s32[]{:T(128)S(6)} %select_n.79), kind=kOutput, calls=%fused_computation.5.clone.1 | convolution fusion | flops 551551488 | bytes 10633732 | tf_op jit(solution)/shard_map/while/body/eval_jaxpr/sub | solution.py:58
  106.8 1.6 dynamic_update_slice.13
  111.2 8.6 %fusion.72 = f32[4,128,4096]{1,2,0:T(8,128)} fusion(pred[128,4096]{0,1:T(8,128)(4,1)S(1)} %compare_and_fusion.2, bf16[128,4,128]{0,2,1:T(8,128)(2,1)S(1)} %bitcast.69, bf16[4096,1024]{1,0:T(8,128)(2,1)} %get-tuple-element.300, s32[]{:T(128)S(6)} %select_n.79), kind=kOutput, calls=%fused_computation.2.clone.1 | convolution fusion | flops 545268736 | bytes 10616836 | tf_op jit(solution)/shard_map/while/body/eval_jaxpr/div | solution.py:60
  119.8 8.4 %multiply_reduce_fusion.2 = f32[4096]{0:T(1024)S(1)} fusion(f32[4,128,4096]{1,2,0:T(8,128)} %fusion.72, f32[128]{0:T(128)S(1)} %compare_convert_fusion.3, pred[128,4096]{0,1:T(8,128)(4,1)S(1)} %compare_and_fusion.2, bf16[128,4,128]{0,2,1:T(8,128)(2,1)S(1)} %bitcast.70, bf16[4096,1024]{1,0:T(8,128)(2,1)} %get-tuple-element.300, s32[]{:T(128)S(6)} %select_n.79), kind=kOutput, calls=%fused_computation.5.clone.1 | convolution fusion | flops 551551488 | bytes 10633732 | tf_op jit(solution)/shard_map/while/body/eval_jaxpr/sub | solution.py:58
  128.2 1.6 dynamic_update_slice.13
  132.5 8.6 %fusion.72 = f32[4,128,4096]{1,2,0:T(8,128)} fusion(pred[128,4096]{0,1:T(8,128)(4,1)S(1)} %compare_and_fusion.2, bf16[128,4,128]{0,2,1:T(8,128)(2,1)S(1)} %bitcast.69, bf16[4096,1024]{1,0:T(8,128)(2,1)} %get-tuple-element.300, s32[]{:T(128)S(6)} %select_n.79), kind=kOutput, calls=%fused_computation.2.clone.1 | convolution fusion | flops 545268736 | bytes 10616836 | tf_op jit(solution)/shard_map/while/body/eval_jaxpr/div | solution.py:60
  141.2 8.4 %multiply_reduce_fusion.2 = f32[4096]{0:T(1024)S(1)} fusion(f32[4,128,4096]{1,2,0:T(8,128)} %fusion.72, f32[128]{0:T(128)S(1)} %compare_convert_fusion.3, pred[128,4096]{0,1:T(8,128)(4,1)S(1)} %compare_and_fusion.2, bf16[128,4,128]{0,2,1:T(8,128)(2,1)S(1)} %bitcast.70, bf16[4096,1024]{1,0:T(8,128)(2,1)} %get-tuple-element.300, s32[]{:T(128)S(6)} %select_n.79), kind=kOutput, calls=%fused_computation.5.clone.1 | convolution fusion | flops 551551488 | bytes 10633732 | tf_op jit(solution)/shard_map/while/body/eval_jaxpr/sub | solution.py:58
  149.6 1.6 dynamic_update_slice.13
  153.9 8.6 %fusion.72 = f32[4,128,4096]{1,2,0:T(8,128)} fusion(pred[128,4096]{0,1:T(8,128)(4,1)S(1)} %compare_and_fusion.2, bf16[128,4,128]{0,2,1:T(8,128)(2,1)S(1)} %bitcast.69, bf16[4096,1024]{1,0:T(8,128)(2,1)} %get-tuple-element.300, s32[]{:T(128)S(6)} %select_n.79), kind=kOutput, calls=%fused_computation.2.clone.1 | convolution fusion | flops 545268736 | bytes 10616836 | tf_op jit(solution)/shard_map/while/body/eval_jaxpr/div | solution.py:60
  162.5 8.4 %multiply_reduce_fusion.2 = f32[4096]{0:T(1024)S(1)} fusion(f32[4,128,4096]{1,2,0:T(8,128)} %fusion.72, f32[128]{0:T(128)S(1)} %compare_convert_fusion.3, pred[128,4096]{0,1:T(8,128)(4,1)S(1)} %compare_and_fusion.2, bf16[128,4,128]{0,2,1:T(8,128)(2,1)S(1)} %bitcast.70, bf16[4096,1024]{1,0:T(8,128)(2,1)} %get-tuple-element.300, s32[]{:T(128)S(6)} %select_n.79), kind=kOutput, calls=%fused_computation.5.clone.1 | convolution fusion | flops 551551488 | bytes 10633732 | tf_op jit(solution)/shard_map/while/body/eval_jaxpr/sub | solution.py:58
  171.0 1.6 dynamic_update_slice.13
  175.3 8.6 %fusion.72 = f32[4,128,4096]{1,2,0:T(8,128)} fusion(pred[128,4096]{0,1:T(8,128)(4,1)S(1)} %compare_and_fusion.2, bf16[128,4,128]{0,2,1:T(8,128)(2,1)S(1)} %bitcast.69, bf16[4096,1024]{1,0:T(8,128)(2,1)} %get-tuple-element.300, s32[]{:T(128)S(6)} %select_n.79), kind=kOutput, calls=%fused_computation.2.clone.1 | convolution fusion | flops 545268736 | bytes 10616836 | tf_op jit(solution)/shard_map/while/body/eval_jaxpr/div | solution.py:60
  183.9 8.4 %multiply_reduce_fusion.2 = f32[4096]{0:T(1024)S(1)} fusion(f32[4,128,4096]{1,2,0:T(8,128)} %fusion.72, f32[128]{0:T(128)S(1)} %compare_convert_fusion.3, pred[128,4096]{0,1:T(8,128)(4,1)S(1)} %compare_and_fusion.2, bf16[128,4,128]{0,2,1:T(8,128)(2,1)S(1)} %bitcast.70, bf16[4096,1024]{1,0:T(8,128)(2,1)} %get-tuple-element.300, s32[]{:T(128)S(6)} %select_n.79), kind=kOutput, calls=%fused_computation.5.clone.1 | convolution fusion | flops 551551488 | bytes 10633732 | tf_op jit(solution)/shard_map/while/body/eval_jaxpr/sub | solution.py:58
  196.7 8.6 %fusion.72 = f32[4,128,4096]{1,2,0:T(8,128)} fusion(pred[128,4096]{0,1:T(8,128)(4,1)S(1)} %compare_and_fusion.2, bf16[128,4,128]{0,2,1:T(8,128)(2,1)S(1)} %bitcast.69, bf16[4096,1024]{1,0:T(8,128)(2,1)} %get-tuple-element.300, s32[]{:T(128)S(6)} %select_n.79), kind=kOutput, calls=%fused_computation.2.clone.1 | convolution fusion | flops 545268736 | bytes 10616836 | tf_op jit(solution)/shard_map/while/body/eval_jaxpr/div | solution.py:60
  205.3 8.4 %multiply_reduce_fusion.2 = f32[4096]{0:T(1024)S(1)} fusion(f32[4,128,4096]{1,2,0:T(8,128)} %fusion.72, f32[128]{0:T(128)S(1)} %compare_convert_fusion.3, pred[128,4096]{0,1:T(8,128)(4,1)S(1)} %compare_and_fusion.2, bf16[128,4,128]{0,2,1:T(8,128)(2,1)S(1)} %bitcast.70, bf16[4096,1024]{1,0:T(8,128)(2,1)} %get-tuple-element.300, s32[]{:T(128)S(6)} %select_n.79), kind=kOutput, calls=%fused_computation.5.clone.1 | convolution fusion | flops 551551488 | bytes 10633732 | tf_op jit(solution)/shard_map/while/body/eval_jaxpr/sub | solution.py:58
  213.7 1.6 dynamic_update_slice.13
  218.1 8.6 %fusion.72 = f32[4,128,4096]{1,2,0:T(8,128)} fusion(pred[128,4096]{0,1:T(8,128)(4,1)S(1)} %compare_and_fusion.2, bf16[128,4,128]{0,2,1:T(8,128)(2,1)S(1)} %bitcast.69, bf16[4096,1024]{1,0:T(8,128)(2,1)} %get-tuple-element.300, s32[]{:T(128)S(6)} %select_n.79), kind=kOutput, calls=%fused_computation.2.clone.1 | convolution fusion | flops 545268736 | bytes 10616836 | tf_op jit(solution)/shard_map/while/body/eval_jaxpr/div | solution.py:60
  226.7 8.4 %multiply_reduce_fusion.2 = f32[4096]{0:T(1024)S(1)} fusion(f32[4,128,4096]{1,2,0:T(8,128)} %fusion.72, f32[128]{0:T(128)S(1)} %compare_convert_fusion.3, pred[128,4096]{0,1:T(8,128)(4,1)S(1)} %compare_and_fusion.2, bf16[128,4,128]{0,2,1:T(8,128)(2,1)S(1)} %bitcast.70, bf16[4096,1024]{1,0:T(8,128)(2,1)} %get-tuple-element.300, s32[]{:T(128)S(6)} %select_n.79), kind=kOutput, calls=%fused_computation.5.clone.1 | convolution fusion | flops 551551488 | bytes 10633732 | tf_op jit(solution)/shard_map/while/body/eval_jaxpr/sub | solution.py:58
  236.7 5.5 all-to-all-start
  242.5 6.5 multiply_convert_fusion
  251.3 2.3 broadcast.49
  255.2 13.2 %fusion.46 = f32[6144,1024]{1,0:T(8,128)} fusion(bf16[128,1024]{1,0:T(8,128)(2,1)S(1)} %get-tuple-element.212, bf16[128,1024]{0,1:T(8,128)(2,1)S(1)} %bitcast.74, bf16[128,1024]{0,1:T(8,128)(2,1)S(1)} %bitcast.72, bf16[128,4096]{0,1:T(8,128)(2,1)S(1)} %get-tuple-element.318), kind=kOutput, calls=%fused_computation.40 | convolution fusion | flops 1615331328 | bytes 27000832 | tf_op jit(solution)/shard_map/dot_general | solution.py:92
  268.4 142.8 %all-reduce.3.cloned.1.call-done = f32[1180672]{0:T(1024)} async-done(((f32[1180672]{0:T(1024)}), f32[1180672]{0:T(1024)}) %all-reduce.3.cloned.1.call-update) | async-done | bytes 4722704
  411.2 7.4 %reshape.90 = f32[128,9224]{1,0:T(8,128)} reshape(f32[1180672]{0:T(1024)} %all-reduce.3.cloned.1.call-done) | data formatting | bytes 9445376 | tf_op jit(solution)/shard_map/all_gather | solution.py:23
  418.7 2.6 reduce_sum.71
  423.5 239.9 %reduce-scatter.2.cloned.1.call-done = f32[48,1024]{1,0:T(8,128)} async-done(((f32[6144,1024]{1,0:T(8,128)}), f32[48,1024]{1,0:T(8,128)}) %reduce-scatter.2.cloned.1.call-update) | async-done | bytes 196624 | tf_op jit(solution)/shard_map/reduce_scatter | solution.py:91
  (60 shorter events, 38.4 us)
Async XLA Ops:
  7.2 242.9 %copy-start = (bf16[1024,8]{0,1:T(8,128)(2,1)S(1)}, bf16[1024,8]{0,1:T(8,128)(2,1)}, u32[]{:S(2)}) copy-start(bf16[1024,8]{0,1:T(8,128)(2,1)} %param.18) | copy-start | bytes 49156
  7.2 58.5 %all-gather.4.cloned.1.call-start = ((), (), s32[]{:S(2)}) async-start(), calls=%async_computation.3 | async-start | bytes 8650752 | tf_op jit(solution)/shard_map/all_gather | solution.py:36
  65.7 176.8 %copy-start.1 = (f32[1024]{0:T(1024)S(1)}, f32[1024]{0:T(1024)}, u32[]{:S(2)}) copy-start(f32[1024]{0:T(1024)} %param.17) | copy-start | bytes 12292
  236.7 13.3 %all-to-all-start = ((f32[32,8,128]{2,1,0:T(8,128)}), f32[32,8,128]{2,1,0:T(8,128)S(1)}, u32[]{:S(2)}, u32[]{:S(2)}) async-start(f32[32,8,128]{2,1,0:T(8,128)} %bitcast.9), calls=%async_computation | async-start | bytes 262144 | tf_op jit(solution)/shard_map/all_to_all | solution.py:15
  242.2 169.0 %all-reduce.3.cloned.1.call-start = ((), (), s32[]{:S(2)}) async-start(), calls=%async_computation.4 | async-start | bytes 9445376
  242.5 7.6 %copy-start.2 = (f32[8]{0:T(128)S(1)}, f32[8]{0:T(128)}, u32[]{:S(2)}) copy-start(f32[8]{0:T(128)} %param.19) | copy-start | bytes 100
  255.1 408.3 %reduce-scatter.2.cloned.1.call-start = ((), (), s32[]{:S(2)}) async-start(), calls=%async_computation.2 | async-start | bytes 25362432 | tf_op jit(solution)/shard_map/reduce_scatter | solution.py:91
Sparse Core Ops, SparseCore 0:
  10.3 55.3 all-gather.3
  255.2 155.9 all-reduce.2
  417.1 246.2 reduce-scatter.1
